TPU v7x, 32 devices: a whole 2x2x4 slice. The times are simulated.
32 devices in a mesh: dom: 8 (over y, x, core), col: 4 (over z).
Axes of the slice: x: 2, y: 2, z: 4, core: 2. Of those that a mesh axis runs over, the one named last changes fastest.
Arguments:
- features: bfloat16 [65536, 1024], P('dom', 'col')
- weight: bfloat16 [1024, 1024], P(None, 'col'), may hold values from -0.1875 to 0.1875
- out_bias: bfloat16 [1024], P('col'), may hold values from -3 to 3
- local_index: int32 [8, 64, 4], P('dom'), may hold values from 0 to 63
- local_count: int32 [8, 64], P('dom'), may hold values from 1 to 4, as said below
- local_vals: bfloat16 [8, 64, 4, 128, 128], P('dom'), may hold values from -0.1875 to 0.1875
- halo_index: int32 [8, 64, 4], P('dom'), may hold values from 0 to 31
- halo_count: int32 [8, 64], P('dom'), may hold values from 0 to 4, as said below
- halo_vals: bfloat16 [8, 64, 4, 128, 128], P('dom'), may hold values from -0.1875 to 0.1875
- send_rows: int32 [8, 8, 512], P('dom'), may hold values from 0 to 8191
- send_count: int32 [8, 8], P('dom'), may hold values from 0 to 512, as said below
Outputs:
- normalized: bfloat16 [65536, 1024], P('dom', 'col')
- channel_stats: float32 [2, 1024], P(None, 'col')
Inputs may be any that keep to these rules, and one draw needn't show every extreme that they name: `local_index`: slots k >= local_count of a row tile are not used. `local_count`: every partition has a row tile with all 4 slots used. `halo_index`: slots k >= halo_count of a row tile are not used. `halo_count`: every partition has a row tile with all 4 slots used. `send_rows`: slots s >= send_count[q, p] are not used. send_count[p, p] is 0; every partition fills all 512 slots to some other partition.
All inputs are finite; a program needn't handle non-finite values.
Results may differ from a plain program's by a relative error of at most 0.0075.
Values may be sent and summed in bfloat16 or wider, within the bound.
A program may use at most 192 MiB of HBM per device.

v0:
```python
import jax
import jax.numpy as jnp
from jax import lax
from jax.sharding import PartitionSpec as P

TILE = 128
epsilon = 1e-06


def tile_sum(sources, tile_index, tile_count, tile_vals):
    gathered = sources[tile_index]
    keep_mask = jnp.arange(tile_vals.shape[1])[None, :] < tile_count[:, None]
    masked = jnp.where(keep_mask[:, :, None, None], tile_vals, jnp.zeros_like(tile_vals))
    return jnp.einsum("tkij,tkjc->tic", masked, gathered, preferred_element_type=jnp.float32)


def on_device(
    features,
    weight,
    out_bias,
    local_index,
    local_count,
    local_vals,
    halo_index,
    halo_count,
    halo_vals,
    send_rows,
    send_count,
):
    row_count, col_width = features.shape
    peer_count = lax.axis_size("dom")
    slot_total = send_rows.shape[2]
    chosen = features[send_rows[0]]
    keep_mask = jnp.arange(slot_total)[None, :] < send_count[0][:, None]
    outgoing = jnp.where(keep_mask[:, :, None], chosen, jnp.zeros_like(chosen))
    arrived = lax.all_to_all(outgoing, "dom", split_axis=0, concat_axis=0, tiled=True)
    halo_tiles = arrived.reshape(peer_count * slot_total // TILE, TILE, col_width)
    own_tiles = features.reshape(row_count // TILE, TILE, col_width)
    summed = tile_sum(own_tiles, local_index[0], local_count[0], local_vals[0])
    summed = summed + tile_sum(halo_tiles, halo_index[0], halo_count[0], halo_vals[0])
    spread = summed.reshape(row_count, col_width).astype(jnp.bfloat16)
    node_total = row_count * peer_count
    regrouped = lax.all_to_all(spread, "col", split_axis=0, concat_axis=1, tiled=True)
    full_weight, full_bias = (
        lax.all_gather(weight, "col", axis=1, tiled=True),
        lax.all_gather(out_bias.reshape(1, col_width), "col", axis=1, tiled=True),
    )
    mixed_rows = jnp.dot(regrouped, full_weight, preferred_element_type=jnp.float32) + full_bias[
        0
    ].astype(jnp.float32)
    active = jnp.maximum(mixed_rows, 0.0)
    row_power = jnp.mean(active * active, axis=1, keepdims=True)
    scaled = active * lax.rsqrt(row_power + epsilon)
    sum_whole, square_whole = lax.psum(
        (jnp.sum(scaled, axis=0), jnp.sum(scaled * scaled, axis=0)), ("dom", "col")
    )
    normalized = lax.all_to_all(
        scaled.astype(jnp.bfloat16), "col", split_axis=1, concat_axis=0, tiled=True
    )
    column_start = lax.axis_index("col") * col_width
    sum_total = lax.dynamic_slice_in_dim(sum_whole, column_start, col_width, 0)
    square_total = lax.dynamic_slice_in_dim(square_whole, column_start, col_width, 0)
    channel_mean = sum_total / node_total
    channel_var = square_total / node_total - channel_mean * channel_mean
    return (normalized, jnp.stack([channel_mean, channel_var]))


def solution(mesh):
    in_specs = (
        P("dom", "col"),
        P(None, "col"),
        P("col"),
        P("dom", None, None),
        P("dom", None),
        P("dom", None, None, None, None),
        P("dom", None, None),
        P("dom", None),
        P("dom", None, None, None, None),
        P("dom", None, None),
        P("dom", None),
    )
    out_specs = (P("dom", "col"), P(None, "col"))
    return jax.shard_map(
        on_device, mesh=mesh, in_specs=in_specs, out_specs=out_specs, check_vma=False
    )
```

profile of v0, /device:TPU:0, one launch (start us, length us, event | category | flops | bytes accessed | tf_op | source)
XLA Modules:
  0.0 374.6 jit_solution(2426596609186330712)
XLA Ops:
  7.2 0.7 fusion.10
  7.9 0.7 iota_compare_fusion.2
  8.6 15.7 %gather_fusion.1 = bf16[4096,256]{1,0:T(8,128)(2,1)S(1)} fusion(bf16[8192,256]{1,0:T(8,128)(2,1)} %param.11, s32[4096]{0:T(1024)S(1)} %broadcast_clamp_fusion), kind=kCustom, calls=%fused_computation.1 | custom fusion | bytes 4210688 | tf_op jit(solution)/shard_map/gather | solution.py:33
  24.4 0.0 copy-start.1
  24.4 1.7 broadcast_select_fusion
  26.1 5.2 %all-to-all-start = ((bf16[8,512,256]{2,1,0:T(8,128)(2,1)}), bf16[8,512,256]{2,1,0:T(8,128)(2,1)S(1)}, u32[]{:S(2)}, u32[]{:S(2)}) async-start(bf16[8,512,256]{2,1,0:T(8,128)(2,1)} %broadcast_select_fusion), calls=%async_computation | async-start | bytes 4194304 | tf_op jit(solution)/shard_map/all_to_all | solution.py:36
  31.3 0.1 copy.19
  31.4 0.1 reshape.208
  31.5 0.1 copy.18
  31.6 0.1 reshape.192
  31.7 0.0 copy-start.2
  31.7 0.0 copy-start.3
  31.7 12.0 %gather_fusion = bf16[256,128,256]{2,1,0:T(8,128)(2,1)} fusion(bf16[64,128,256]{2,1,0:T(8,128)(2,1)} %bitcast.52, s32[1024]{0:T(1024)S(1)} %pad_clamp_fusion.1), kind=kCustom, calls=%fused_computation | custom fusion | bytes 33555456 | tf_op jit(solution)/shard_map/gather | solution.py:11
  43.7 0.1 iota_compare_fusion
  43.8 0.1 iota_compare_fusion.1
  43.9 14.0 %all-to-all-done = bf16[8,512,256]{2,1,0:T(8,128)(2,1)S(1)} async-done(((bf16[8,512,256]{2,1,0:T(8,128)(2,1)}), bf16[8,512,256]{2,1,0:T(8,128)(2,1)S(1)}, u32[]{:S(2)}, u32[]{:S(2)}) %all-to-all-start) | async-done | bytes 2097184 | tf_op jit(solution)/shard_map/all_to_all | solution.py:36
  57.9 9.7 %gather_fusion.2 = bf16[256,128,256]{2,1,0:T(8,128)(2,1)} fusion(bf16[32,128,256]{2,1,0:T(8,128)(2,1)S(1)} %bitcast.53, s32[1024]{0:T(1024)S(1)} %pad_clamp_fusion), kind=kCustom, calls=%fused_computation.2 | custom fusion | bytes 33555456 | tf_op jit(solution)/shard_map/gather | solution.py:11
  67.6 13.8 %fusion.1 = f32[64,128,256,1]{2,1,3,0:T(8,128)} fusion(bf16[64,4,128,256]{3,2,1,0:T(8,128)(2,1)} %bitcast.54, bf16[1,64,4,128,128]{4,3,2,1,0:T(8,128)(2,1)} %param.19, pred[64,4]{1,0:T(8,128)(4,1)S(1)} %iota_compare_fusion), kind=kOutput, calls=%fused_computation.6 | convolution fusion | flops 2151677952 | bytes 33554688 | tf_op jit(solution)/shard_map/tkij,tkjc->tic/dot_general | solution.py:14
  81.4 14.0 %fusion = bf16[64,128,256]{2,1,0:T(8,128)(2,1)} fusion(f32[64,128,256,1]{2,1,3,0:T(8,128)} %fusion.1, bf16[64,4,128,256]{3,2,1,0:T(8,128)(2,1)} %bitcast.55, bf16[1,64,4,128,128]{4,3,2,1,0:T(8,128)(2,1)} %param.16, pred[64,4]{1,0:T(8,128)(4,1)S(1)} %iota_compare_fusion.1), kind=kOutput, calls=%fused_computation.4 | convolution fusion | flops 2155872256 | bytes 37748992 | tf_op jit(solution)/shard_map/tkij,tkjc->tic/dot_general | solution.py:14
  95.4 6.3 %copy.20 = bf16[4,2048,256]{1,2,0:T(8,128)(2,1)} copy(bf16[4,2048,256]{2,1,0:T(8,128)(2,1)} %bitcast.56) | data formatting | bytes 8388608 | tf_op jit(solution)/shard_map/convert_element_type | solution.py:41
  101.6 4.9 %all-to-all-start.1 = ((bf16[4,2048,256]{1,2,0:T(8,128)(2,1)}), bf16[4,2048,256]{1,2,0:T(8,128)(2,1)}, u32[]{:S(2)}, u32[]{:S(2)}) async-start(bf16[4,2048,256]{1,2,0:T(8,128)(2,1)} %copy.20), calls=%async_computation.1 | async-start | bytes 8388608 | tf_op jit(solution)/shard_map/all_to_all | solution.py:43
  106.5 0.0 all-gather.4.cloned.1.call-start
  106.5 0.7 all-gather.4.cloned.1.call-update
  107.3 103.9 %all-gather.1 = bf16[4,1,256]{2,1,0:T(2,128)(2,1)S(1)} all-gather(bf16[1,1,256]{2,1,0:T(2,128)(2,1)S(1)} %reshape.220), channel_id=2, replica_groups=mesh['dom'=8,'col'=4] {'col'}, dimensions={0}, use_global_device_ids=true | all-gather | bytes 2560 | tf_op jit(solution)/shard_map/all_gather | solution.py:46
  211.2 19.8 %all-to-all-done.1 = bf16[4,2048,256]{1,2,0:T(8,128)(2,1)} async-done(((bf16[4,2048,256]{1,2,0:T(8,128)(2,1)}), bf16[4,2048,256]{1,2,0:T(8,128)(2,1)}, u32[]{:S(2)}, u32[]{:S(2)}) %all-to-all-start.1) | async-done | bytes 4194336 | tf_op jit(solution)/shard_map/all_to_all | solution.py:43
  231.0 7.8 %multiply_reduce_fusion.1 = (f32[2048]{0:T(1024)S(1)}, f32[2048,1024]{0,1:T(8,128)S(1)}) fusion(f32[1024]{0:T(1024)S(1)} %bitcast.61, bf16[2048,1024]{0,1:T(8,128)(2,1)} %bitcast.19, bf16[1024,1024]{1,0:T(8,128)(2,1)} %all-gather.4.cloned.1.call-done), kind=kOutput, calls=%fused_computation.10 | convolution fusion | flops 4303353856 | bytes 14692352 | tf_op jit(solution)/shard_map/dot_general | solution.py:48
  238.8 3.5 fusion.6
  242.2 4.8 %all-to-all-start.2 = ((bf16[2048,4,256]{0,2,1:T(8,128)(2,1)}), bf16[2048,4,256]{0,2,1:T(8,128)(2,1)}, u32[]{:S(2)}, u32[]{:S(2)}) async-start(bf16[2048,4,256]{0,2,1:T(8,128)(2,1)} %bitcast.57), calls=%async_computation.2 | async-start | bytes 8388608 | tf_op jit(solution)/shard_map/all_to_all | solution.py:57
  247.1 113.8 %all-reduce = (f32[1024]{0:T(1024)S(1)}, f32[1024]{0:T(1024)S(1)}) all-reduce(f32[1024]{0:T(1024)S(1)} %get-tuple-element.3, f32[1024]{0:T(1024)S(1)} %get-tuple-element.2), channel_id=1, replica_groups=mesh['dom'=8,'col'=4] {'dom','col'}, use_global_device_ids=true, to_apply=%region_4.5 | all-reduce | flops 2048 | bytes 16384 | tf_op jit(solution)/shard_map/psum | solution.py:54
  360.9 0.1 dynamic-slice_multiply_fusion
  361.0 0.6 pad_maximum_fusion
  361.6 6.2 %copy.21 = bf16[4,2048,256]{2,1,0:T(8,128)(2,1)} copy(bf16[4,2048,256]{1,2,0:T(8,128)(2,1)} %bitcast.22) | data formatting | bytes 8388608 | tf_op jit(solution)/shard_map/all_to_all | solution.py:57
  (18 shorter events, 0.1 us)
Async XLA Ops:
  24.4 6.9 %copy-start = (s32[1,64,4]{1,2,0:T(4,128)S(1)}, s32[1,64,4]{1,2,0:T(4,128)}, u32[]{:S(2)}) copy-start(s32[1,64,4]{1,2,0:T(4,128)} %param.17) | copy-start | bytes 3076
  24.4 7.1 %copy-start.1 = (s32[1,64,4]{1,2,0:T(4,128)S(1)}, s32[1,64,4]{1,2,0:T(4,128)}, u32[]{:S(2)}) copy-start(s32[1,64,4]{1,2,0:T(4,128)} %param.14) | copy-start | bytes 3076
  26.1 31.8 %all-to-all-start = ((bf16[8,512,256]{2,1,0:T(8,128)(2,1)}), bf16[8,512,256]{2,1,0:T(8,128)(2,1)S(1)}, u32[]{:S(2)}, u32[]{:S(2)}) async-start(bf16[8,512,256]{2,1,0:T(8,128)(2,1)} %broadcast_select_fusion), calls=%async_computation | async-start | bytes 4194304 | tf_op jit(solution)/shard_map/all_to_all | solution.py:36
  31.7 12.0 %copy-start.2 = (s32[1,64]{1,0:T(1,128)S(1)}, s32[1,64]{1,0:T(1,128)}, u32[]{:S(2)}) copy-start(s32[1,64]{1,0:T(1,128)} %param.18) | copy-start | bytes 772
  31.7 12.1 %copy-start.3 = (s32[1,64]{1,0:T(1,128)S(1)}, s32[1,64]{1,0:T(1,128)}, u32[]{:S(2)}) copy-start(s32[1,64]{1,0:T(1,128)} %param.15) | copy-start | bytes 772
  95.4 11.9 %copy-start.4 = (bf16[256]{0:T(256)(128)(2,1)S(1)}, bf16[256]{0:T(256)(128)(2,1)}, u32[]{:S(2)}) copy-start(bf16[256]{0:T(256)(128)(2,1)} %param.13) | copy-start | bytes 1540
  101.6 129.3 %all-to-all-start.1 = ((bf16[4,2048,256]{1,2,0:T(8,128)(2,1)}), bf16[4,2048,256]{1,2,0:T(8,128)(2,1)}, u32[]{:S(2)}, u32[]{:S(2)}) async-start(bf16[4,2048,256]{1,2,0:T(8,128)(2,1)} %copy.20), calls=%async_computation.1 | async-start | bytes 8388608 | tf_op jit(solution)/shard_map/all_to_all | solution.py:43
  106.5 104.7 %all-gather.4.cloned.1.call-start = ((), (), s32[]{:S(2)}) async-start(), calls=%async_computation.3 | async-start | bytes 2621440 | tf_op jit(solution)/shard_map/all_gather | solution.py:45
  242.2 119.3 %all-to-all-start.2 = ((bf16[2048,4,256]{0,2,1:T(8,128)(2,1)}), bf16[2048,4,256]{0,2,1:T(8,128)(2,1)}, u32[]{:S(2)}, u32[]{:S(2)}) async-start(bf16[2048,4,256]{0,2,1:T(8,128)(2,1)} %bitcast.57), calls=%async_computation.2 | async-start | bytes 8388608 | tf_op jit(solution)/shard_map/all_to_all | solution.py:57
Sparse Core Ops, SparseCore 0:
  108.9 94.7 all-gather.3
where the time goes:
time: 375 us
  blocking collectives  218 us (58%)
  local copies, waits for them, and re-layouts  50.3 us (13%)
  matrix products  35.5 us (9%)
  waiting for transfers between devices  34.5 us (9%)
  starting transfers between devices  14.9 us (4%)
  between operations  14.2 us (4%)
  other arithmetic  7.48 us (2%)
    psum x1, blocking collectives, on_device(): lax.psum((jnp.sum(scaled, axis=0), jnp.sum(scaled * scaled, axis=0)), ('d...  114 us
    all_gather x1, blocking collectives, on_device(): lax.all_gather(out_bias.reshape(1, col_width), 'col', axis=1, tiled=True)  104 us
    dot_general x2, matrix products, tile_sum(): jnp.einsum('tkij,tkjc->tic', masked, gathered, preferred_element_type=jnp...  27.7 us
    gather x2, local copies, waits for them, and re-layouts, tile_sum(): gathered = sources[tile_index]  21.7 us
    all_to_all x1, waiting for transfers between devices, on_device(): lax.all_to_all(spread, 'col', split_axis=0, concat_axis=1, tiled=True)  19.8 us
    gather x1, local copies, waits for them, and re-layouts, on_device(): chosen = features[send_rows[0]]  15.7 us
    all_to_all x1, waiting for transfers between devices, on_device(): lax.all_to_all(outgoing, 'dom', split_axis=0, concat_axis=0, tiled=True)  14 us
    dot_general x1, matrix products, on_device(): jnp.dot(regrouped, full_weight, preferred_element_type=jnp.float32)  7.76 us
  transfers between devices with their start and end apart: 4, of which 2 were waited for; matrix products, arithmetic and copies ran while one was open for 4% of the time, Pallas kernels for 0%

commit v1 on v0

--- a/solution.py
+++ b/solution.py
@@ -40,7 +40,9 @@
     summed = summed + tile_sum(halo_tiles, halo_index[0], halo_count[0], halo_vals[0])
     spread = summed.reshape(row_count, col_width).astype(jnp.bfloat16)
     node_total = row_count * peer_count
-    regrouped = lax.all_to_all(spread, "col", split_axis=0, concat_axis=1, tiled=True)
+    parts = jnp.split(spread, lax.axis_size("col"), axis=0)
+    received = lax.all_to_all(jnp.stack(parts), "col", 0, 0)
+    regrouped = jnp.concatenate(received, axis=1)
     full_weight, full_bias = (
         lax.all_gather(weight, "col", axis=1, tiled=True),
         lax.all_gather(out_bias.reshape(1, col_width), "col", axis=1, tiled=True),

time: 375 us -> 378 us (level)
    convert_element_type x1 -> x0, local copies, waits for them, and re-layouts: 6.27 us -> none  [on_device(): spread = summed.reshape(row_count, col_width).astype(jnp.bfloat16)]
    another operation x0 -> x4, local copies, waits for them, and re-layouts: none -> 5.82 us  [on_device(): received = lax.all_to_all(jnp.stack(parts), 'col', 0, 0)]
  transfers between devices with their start and end apart: 4 -> 4, of which waited for: 2 -> 2; matrix products, arithmetic and copies ran while one was open for 4% -> 3% of each run, Pallas kernels for 0% -> 0%
where the time goes in v1:
time: 378 us; the launch traced here: 377 us
  blocking collectives  218 us (58%)
  local copies, waits for them, and re-layouts  51.5 us (14%)
  waiting for transfers between devices  34.5 us (9%)
  matrix products  33.4 us (9%)
  starting transfers between devices  14.9 us (4%)
  between operations  14.2 us (4%)
  other arithmetic  11 us (3%)
    psum x1, blocking collectives, on_device(): lax.psum((jnp.sum(scaled, axis=0), jnp.sum(scaled * scaled, axis=0)), ('d...  114 us
    all_gather x1, blocking collectives, on_device(): lax.all_gather(out_bias.reshape(1, col_width), 'col', axis=1, tiled=True)  104 us
    dot_general x2, matrix products, tile_sum(): jnp.einsum('tkij,tkjc->tic', masked, gathered, preferred_element_type=jnp...  25.7 us
    gather x2, local copies, waits for them, and re-layouts, tile_sum(): gathered = sources[tile_index]  21.7 us
    all_to_all x1, waiting for transfers between devices, on_device(): received = lax.all_to_all(jnp.stack(parts), 'col', 0, 0)  19.8 us
    gather x1, local copies, waits for them, and re-layouts, on_device(): chosen = features[send_rows[0]]  15.7 us
    all_to_all x1, waiting for transfers between devices, on_device(): lax.all_to_all(outgoing, 'dom', split_axis=0, concat_axis=0, tiled=True)  14 us
    dot_general x1, matrix products, on_device(): jnp.dot(regrouped, full_weight, preferred_element_type=jnp.float32)  7.76 us
  transfers between devices with their start and end apart: 4, of which 2 were waited for; matrix products, arithmetic and copies ran while one was open for 3% of the time, Pallas kernels for 0%

profile of v1, /device:TPU:0, one launch (start us, length us, event | category | flops | bytes accessed | tf_op | source)
XLA Modules:
  0.0 377.2 jit_solution(7002946910222332254)
XLA Ops:
  7.2 0.7 fusion.10
  7.9 0.7 iota_compare_fusion.2
  8.6 15.7 %gather_fusion.1 = bf16[4096,256]{1,0:T(8,128)(2,1)S(1)} fusion(bf16[8192,256]{1,0:T(8,128)(2,1)} %param.11, s32[4096]{0:T(1024)S(1)} %broadcast_clamp_fusion), kind=kCustom, calls=%fused_computation.1 | custom fusion | bytes 4210688 | tf_op jit(solution)/shard_map/gather | solution.py:33
  24.4 1.7 broadcast_select_fusion
  26.1 5.2 %all-to-all-start = ((bf16[8,512,256]{2,1,0:T(8,128)(2,1)}), bf16[8,512,256]{2,1,0:T(8,128)(2,1)S(1)}, u32[]{:S(2)}, u32[]{:S(2)}) async-start(bf16[8,512,256]{2,1,0:T(8,128)(2,1)} %broadcast_select_fusion), calls=%async_computation | async-start | bytes 4194304 | tf_op jit(solution)/shard_map/all_to_all | solution.py:36
  31.3 0.1 copy.22
  31.4 0.1 reshape.220
  31.5 0.1 copy.21
  31.6 0.1 reshape.204
  31.7 12.0 %gather_fusion = bf16[256,128,256]{2,1,0:T(8,128)(2,1)} fusion(bf16[64,128,256]{2,1,0:T(8,128)(2,1)} %bitcast.55, s32[1024]{0:T(1024)S(1)} %pad_clamp_fusion.1), kind=kCustom, calls=%fused_computation | custom fusion | bytes 33555456 | tf_op jit(solution)/shard_map/gather | solution.py:11
  43.7 0.1 iota_compare_fusion
  43.9 14.0 %all-to-all-done = bf16[8,512,256]{2,1,0:T(8,128)(2,1)S(1)} async-done(((bf16[8,512,256]{2,1,0:T(8,128)(2,1)}), bf16[8,512,256]{2,1,0:T(8,128)(2,1)S(1)}, u32[]{:S(2)}, u32[]{:S(2)}) %all-to-all-start) | async-done | bytes 2097184 | tf_op jit(solution)/shard_map/all_to_all | solution.py:36
  57.9 9.7 %gather_fusion.2 = bf16[256,128,256]{2,1,0:T(8,128)(2,1)} fusion(bf16[32,128,256]{2,1,0:T(8,128)(2,1)S(1)} %bitcast.56, s32[1024]{0:T(1024)S(1)} %pad_clamp_fusion), kind=kCustom, calls=%fused_computation.2 | custom fusion | bytes 33555456 | tf_op jit(solution)/shard_map/gather | solution.py:11
  67.6 13.8 %fusion.1 = f32[64,128,256,1]{2,1,3,0:T(8,128)} fusion(bf16[64,4,128,256]{3,2,1,0:T(8,128)(2,1)} %bitcast.57, bf16[1,64,4,128,128]{4,3,2,1,0:T(8,128)(2,1)} %param.19, pred[64,4]{1,0:T(8,128)(4,1)S(1)} %iota_compare_fusion), kind=kOutput, calls=%fused_computation.6 | convolution fusion | flops 2151677952 | bytes 33554688 | tf_op jit(solution)/shard_map/tkij,tkjc->tic/dot_general | solution.py:14
  81.4 11.9 %fusion = bf16[64,128,256]{2,1,0:T(8,128)(2,1)S(1)} fusion(f32[64,128,256,1]{2,1,3,0:T(8,128)} %fusion.1, bf16[64,4,128,256]{3,2,1,0:T(8,128)(2,1)} %bitcast.58, bf16[1,64,4,128,128]{4,3,2,1,0:T(8,128)(2,1)} %param.16, pred[64,4]{1,0:T(8,128)(4,1)S(1)} %iota_compare_fusion.1), kind=kOutput, calls=%fused_computation.4 | convolution fusion | flops 2155872256 | bytes 37748992 | tf_op jit(solution)/shard_map/tkij,tkjc->tic/dot_general | solution.py:14
  93.3 1.6 fusion.13
  94.9 1.5 copy.23
  96.4 2.3 copy.24
  98.7 1.4 copy.25
  100.1 0.6 copy.26
  100.8 3.5 pad_maximum_fusion
  104.3 4.9 %all-to-all-start.1 = ((bf16[4,2048,256]{1,2,0:T(8,128)(2,1)}), bf16[4,2048,256]{1,2,0:T(8,128)(2,1)}, u32[]{:S(2)}, u32[]{:S(2)}) async-start(bf16[4,2048,256]{1,2,0:T(8,128)(2,1)} %pad_maximum_fusion), calls=%async_computation.1 | async-start | bytes 8388608 | tf_op jit(solution)/shard_map/all_to_all | solution.py:44
  109.2 0.7 all-gather.4.cloned.1.call-update
  109.9 103.9 %all-gather.1 = bf16[4,1,256]{2,1,0:T(2,128)(2,1)S(1)} all-gather(bf16[1,1,256]{2,1,0:T(2,128)(2,1)S(1)} %reshape.232), channel_id=2, replica_groups=mesh['dom'=8,'col'=4] {'col'}, dimensions={0}, use_global_device_ids=true | all-gather | bytes 2560 | tf_op jit(solution)/shard_map/all_gather | solution.py:48
  213.8 19.8 %all-to-all-done.1 = bf16[4,2048,256]{1,2,0:T(8,128)(2,1)} async-done(((bf16[4,2048,256]{1,2,0:T(8,128)(2,1)}), bf16[4,2048,256]{1,2,0:T(8,128)(2,1)}, u32[]{:S(2)}, u32[]{:S(2)}) %all-to-all-start.1) | async-done | bytes 4194336 | tf_op jit(solution)/shard_map/all_to_all | solution.py:44
  233.6 7.8 %multiply_reduce_fusion.1 = (f32[2048]{0:T(1024)S(1)}, f32[2048,1024]{0,1:T(8,128)S(1)}) fusion(f32[1024]{0:T(1024)S(1)} %bitcast.67, bf16[2048,1024]{0,1:T(8,128)(2,1)} %bitcast.22, bf16[1024,1024]{1,0:T(8,128)(2,1)} %all-gather.4.cloned.1.call-done), kind=kOutput, calls=%fused_computation.10 | convolution fusion | flops 4303353856 | bytes 14692352 | tf_op jit(solution)/shard_map/dot_general | solution.py:50
  241.4 3.5 fusion.6
  244.9 4.8 %all-to-all-start.2 = ((bf16[2048,4,256]{0,2,1:T(8,128)(2,1)}), bf16[2048,4,256]{0,2,1:T(8,128)(2,1)}, u32[]{:S(2)}, u32[]{:S(2)}) async-start(bf16[2048,4,256]{0,2,1:T(8,128)(2,1)} %bitcast.59), calls=%async_computation.2 | async-start | bytes 8388608 | tf_op jit(solution)/shard_map/all_to_all | solution.py:59
  249.7 113.8 %all-reduce = (f32[1024]{0:T(1024)S(1)}, f32[1024]{0:T(1024)S(1)}) all-reduce(f32[1024]{0:T(1024)S(1)} %get-tuple-element.3, f32[1024]{0:T(1024)S(1)} %get-tuple-element.2), channel_id=1, replica_groups=mesh['dom'=8,'col'=4] {'dom','col'}, use_global_device_ids=true, to_apply=%region_4.5 | all-reduce | flops 2048 | bytes 16384 | tf_op jit(solution)/shard_map/psum | solution.py:56
  363.5 0.1 dynamic-slice_multiply_fusion
  363.6 0.6 pad_maximum_fusion.1
  364.2 6.2 %copy.27 = bf16[4,2048,256]{2,1,0:T(8,128)(2,1)} copy(bf16[4,2048,256]{1,2,0:T(8,128)(2,1)} %bitcast.25) | data formatting | bytes 8388608 | tf_op jit(solution)/shard_map/all_to_all | solution.py:59
  (23 shorter events, 0.2 us)
Async XLA Ops:
  24.4 6.9 %copy-start = (s32[1,64,4]{1,2,0:T(4,128)S(1)}, s32[1,64,4]{1,2,0:T(4,128)}, u32[]{:S(2)}) copy-start(s32[1,64,4]{1,2,0:T(4,128)} %param.17) | copy-start | bytes 3076
  24.4 7.1 %copy-start.1 = (s32[1,64,4]{1,2,0:T(4,128)S(1)}, s32[1,64,4]{1,2,0:T(4,128)}, u32[]{:S(2)}) copy-start(s32[1,64,4]{1,2,0:T(4,128)} %param.14) | copy-start | bytes 3076
  26.1 31.8 %all-to-all-start = ((bf16[8,512,256]{2,1,0:T(8,128)(2,1)}), bf16[8,512,256]{2,1,0:T(8,128)(2,1)S(1)}, u32[]{:S(2)}, u32[]{:S(2)}) async-start(bf16[8,512,256]{2,1,0:T(8,128)(2,1)} %broadcast_select_fusion), calls=%async_computation | async-start | bytes 4194304 | tf_op jit(solution)/shard_map/all_to_all | solution.py:36
  31.7 12.0 %copy-start.2 = (s32[1,64]{1,0:T(1,128)S(1)}, s32[1,64]{1,0:T(1,128)}, u32[]{:S(2)}) copy-start(s32[1,64]{1,0:T(1,128)} %param.18) | copy-start | bytes 772
  31.7 12.1 %copy-start.3 = (s32[1,64]{1,0:T(1,128)S(1)}, s32[1,64]{1,0:T(1,128)}, u32[]{:S(2)}) copy-start(s32[1,64]{1,0:T(1,128)} %param.15) | copy-start | bytes 772
  100.8 9.1 %copy-start.4 = (bf16[256]{0:T(256)(128)(2,1)S(1)}, bf16[256]{0:T(256)(128)(2,1)}, u32[]{:S(2)}) copy-start(bf16[256]{0:T(256)(128)(2,1)} %param.13) | copy-start | bytes 1540
  104.3 129.3 %all-to-all-start.1 = ((bf16[4,2048,256]{1,2,0:T(8,128)(2,1)}), bf16[4,2048,256]{1,2,0:T(8,128)(2,1)}, u32[]{:S(2)}, u32[]{:S(2)}) async-start(bf16[4,2048,256]{1,2,0:T(8,128)(2,1)} %pad_maximum_fusion), calls=%async_computation.1 | async-start | bytes 8388608 | tf_op jit(solution)/shard_map/all_to_all | solution.py:44
  109.1 104.7 %all-gather.4.cloned.1.call-start = ((), (), s32[]{:S(2)}) async-start(), calls=%async_computation.3 | async-start | bytes 2621440 | tf_op jit(solution)/shard_map/all_gather | solution.py:47
  244.9 119.3 %all-to-all-start.2 = ((bf16[2048,4,256]{0,2,1:T(8,128)(2,1)}), bf16[2048,4,256]{0,2,1:T(8,128)(2,1)}, u32[]{:S(2)}, u32[]{:S(2)}) async-start(bf16[2048,4,256]{0,2,1:T(8,128)(2,1)} %bitcast.59), calls=%async_computation.2 | async-start | bytes 8388608 | tf_op jit(solution)/shard_map/all_to_all | solution.py:59
Sparse Core Ops, SparseCore 0:
  111.5 94.7 all-gather.3
